TPU v7x, 32 devices: a whole 2x2x4 slice. The times are simulated.
32 devices in a mesh: tm: 8 (over z, y), node: 4 (over x, core).
Axes of the slice: x: 2, y: 2, z: 4, core: 2. Of those that a mesh axis runs over, the one named last changes fastest.
Arguments:
- slice_starts: float32 [8, 32, 16384], P('tm'), may hold values from -1 to 1
- coupling: float32 [32, 16384], replicated, may hold values from 0.03 to 0.25
Outputs:
- node_values: float32 [8, 4, 32, 16384], P('tm', 'node')
- residual_log: float32 [3, 32], replicated
All inputs are finite; a program needn't handle non-finite values.
Results may differ from a plain program's by a relative error of at most 0.0001.
Values sent between devices are 32-bit elements.
A program may use at most 128 MiB of HBM per device.

v0:
```python
import jax
import jax.numpy as jnp
from jax import lax
from jax.sharding import PartitionSpec as P

M = 4
SWEEPS = 3
NEWTON = 2
time_step = 0.5
log_floor = 0.05


def spread(value, axis, root):
    mine = lax.axis_index(axis) == root
    return lax.psum(jnp.where(mine, value, jnp.zeros_like(value)), axis)


def passed_along(value, axis, by):
    size = lax.axis_size(axis)
    pairs = [(i, i + by) for i in range(size) if 0 <= i + by < size]
    return lax.ppermute(value, axis, pairs)


def legendre_gap(point, node_count):
    before = 1.0
    current = point
    for degree in range(1, node_count):
        following = ((2 * degree + 1) * point * current - degree * before) / (degree + 1)
        before = current
        current = following
    return current - before


def collocation(node_count):
    points = []
    samples = 4000
    for sample_index in range(samples - 1):
        lower_end = -1.0 + 2.0 * sample_index / samples
        upper_end = -1.0 + 2.0 * (sample_index + 1) / samples
        lower_value = legendre_gap(lower_end, node_count)
        upper_value = legendre_gap(upper_end, node_count)
        if lower_value * upper_value < 0.0:
            for halving in range(80):
                middle = 0.5 * (lower_end + upper_end)
                middle_value = legendre_gap(middle, node_count)
                if lower_value * middle_value <= 0.0:
                    upper_end = middle
                else:
                    lower_end = middle
                    lower_value = middle_value
            points.append(0.5 * (lower_end + upper_end))
    points.append(1.0)
    node_times = [(point + 1.0) / 2.0 for point in points]
    matrix = [[0.0] * node_count for row_index in range(node_count)]
    for column in range(node_count):
        coeffs = [1.0]
        for other in range(node_count):
            if other != column:
                scale = node_times[column] - node_times[other]
                shifted = [0.0] + coeffs
                scaled = [value * node_times[other] for value in coeffs] + [0.0]
                coeffs = [(shifted[power] - scaled[power]) / scale for power in range(len(shifted))]
        for row_index in range(node_count):
            upper_time = node_times[row_index]
            matrix[row_index][column] = sum(
                (
                    coeffs[power] * upper_time ** (power + 1) / (power + 1)
                    for power in range(len(coeffs))
                )
            )
    return (node_times, matrix)


def operator_term(field_values, coupling):
    right_side = jnp.roll(field_values, -1, axis=-1)
    left_side = jnp.roll(field_values, 1, axis=-1)
    left_coupling = jnp.roll(coupling, 1, axis=-1)
    cubic = field_values * field_values * field_values
    return (
        coupling * (right_side - field_values)
        - left_coupling * (field_values - left_side)
        + field_values
        - cubic
    )


def body(slice_starts, coupling):
    node_times, matrix = collocation(M)
    weights = jnp.asarray(matrix, jnp.float32)
    diag_weights = jnp.asarray([time_step * moment / M for moment in node_times], jnp.float32)
    node_pos = lax.axis_index("node")
    slice_pos = lax.axis_index("tm")
    systems, cells = coupling.shape
    initial = slice_starts[0]
    implicit = diag_weights[node_pos]
    row_weights = weights[node_pos]
    node_state = initial
    totals = []
    for sweep_index in range(SWEEPS):
        if sweep_index == 0:
            end_value = initial
        else:
            end_value = spread(node_state, "node", M - 1)
        arrived = passed_along(end_value, "tm", 1)
        start_value = jnp.where(slice_pos == 0, initial, arrived)
        forcing = operator_term(node_state, coupling)
        segment = lax.all_gather(forcing, "node", axis=0, tiled=True)
        positions = jnp.arange(segment.shape[0], dtype=jnp.int32)
        owners = positions // systems
        members = positions % systems
        factors = jnp.sum(
            jnp.where(
                owners[:, None] == jnp.arange(M, dtype=jnp.int32)[None], row_weights[None], 0.0
            ),
            axis=1,
        )
        select = jnp.where(
            jnp.arange(systems, dtype=jnp.int32)[:, None] == members[None], factors[None], 0.0
        )
        quadrature = jnp.zeros_like(forcing) + jnp.dot(
            select, segment, precision=lax.Precision.HIGHEST
        )
        base = start_value + time_step * quadrature
        defect = base - node_state
        partial_value = jnp.sum(defect * defect, axis=1)
        totals.append(lax.psum(partial_value, ("tm", "node")))
        target = base - implicit * (node_state - node_state * node_state * node_state)
        iterate = node_state
        for newton_step in range(NEWTON):
            cubic = iterate * iterate * iterate
            derivative = 1.0 - implicit + 3.0 * implicit * iterate * iterate
            iterate = iterate - (iterate - implicit * (iterate - cubic) - target) / derivative
        node_state = iterate
    summed = jnp.stack(totals)
    cell_total = lax.axis_size("tm") * M * cells
    residual_log = jnp.log(log_floor + summed / cell_total)
    return (node_state[None, None], residual_log)


def solution(mesh):
    placed = (P("tm", None, None), P())
    return jax.shard_map(
        body,
        mesh=mesh,
        in_specs=placed,
        out_specs=(P("tm", "node", None, None), P()),
        check_vma=False,
    )
```

profile of v0, /device:TPU:0, one launch (start us, length us, event | category | flops | bytes accessed | tf_op | source)
XLA Modules:
  0.0 382.4 jit_solution(9539708886038330631)
XLA Ops:
  7.2 0.0 all-gather.4.cloned.1.call-start
  7.2 0.8 fusion.81
  8.0 0.0 copy-start
  8.0 0.0 copy-start.1
  8.0 3.0 fusion.82
  11.1 0.0 copy-done
  11.1 0.1 slice.52
  11.2 0.4 copy-done.1
  11.5 2.5 fusion
  14.0 0.0 copy-start.5
  14.0 0.0 all-gather.4.cloned.1.call-update
  14.0 0.0 all-reduce.4.cloned.1.call-start
  14.1 6.3 %collective-permute-start = (f32[32,16384]{1,0:T(8,128)}, f32[32,16384]{1,0:T(8,128)}, u32[]{:S(2)}, u32[]{:S(2)}) collective-permute-start(f32[32,16384]{1,0:T(8,128)} %bitcast.26), channel_id=1, source_target_pairs={{0,4},{4,8},{8,12},{12,16},{16,20},{20,24},{24,28},{1,5},{5,9},{9,... | collective-permute-start | bytes 6291464 | tf_op jit(solution)/shard_map/ppermute | solution.py:21
  20.3 0.0 copy-done.5
  20.3 0.6 dynamic_slice.6
  22.2 0.7 dynamic-slice_bitcast_fusion
  22.9 0.1 select_reduce_fusion
  23.0 41.1 %collective-permute-done = f32[32,16384]{1,0:T(8,128)} collective-permute-done((f32[32,16384]{1,0:T(8,128)}, f32[32,16384]{1,0:T(8,128)}, u32[]{:S(2)}, u32[]{:S(2)}) %collective-permute-start) | collective-permute-done | bytes 2097184 | tf_op jit(solution)/shard_map/ppermute | solution.py:21
  64.2 11.0 %all-gather.4.cloned.1.call-done = f32[128,16384]{1,0:T(8,128)} async-done(((f32[32,16384]{1,0:T(8,128)}), f32[128,16384]{1,0:T(8,128)}) %all-gather.4.cloned.1.call-update) | async-done | bytes 8388624 | tf_op jit(solution)/shard_map/all_gather | solution.py:107
  75.2 10.5 %broadcast_select_fusion.1 = (f32[32,16384]{1,0:T(8,128)}, f32[32,16384]{1,0:T(8,128)S(1)}, f32[32]{0:T(128)S(1)}) fusion(pred[]{:T(512)S(6)} %eq.27, f32[]{:T(128)S(6)} %mul.175, f32[]{:T(128)S(6)} %sub.156, f32[32,16384]{1,0:T(8,128)} %collective-permute-done, pred[]{:T(512)S(6)} %eq.20, f32[]{:T(128)} %bitcast.1, f32[1,32,16384]{2,1,0:T(8,128)} %param.4, ...), kind=kOutput, calls=%fused_computation.87 | convolution fusion | flops 821043200 | bytes 16778382 | tf_op jit(solution)/shard_map/dot_general | solution.py:120
  85.6 0.0 copy-start.4
  85.6 0.1 fusion.79
  85.7 2.6 fusion.80
  88.3 0.0 copy-done.4
  88.3 0.0 all-reduce.4.cloned.1.call-update
  88.4 0.0 all-gather.6.cloned.1.call-start
  88.4 5.3 %fusion.2 = f32[32,16384]{1,0:T(8,128)} fusion(f32[32,16384]{1,0:T(8,128)} %copy-done.4, f32[32,16384]{1,0:T(8,128)S(1)} %copy-done, f32[32,1]{1,0:T(8,128)S(1)} %get-tuple-element.18, f32[32,16383]{1,0:T(8,128)} %get-tuple-element.20, f32[32,16383]{1,0:T(8,128)} %get-tuple-element.19, f32[32,1]{1,0:T(8,128)S(1)} %get-tuple-element.17, ...), kind=kLoop, calls=%fused_computation.17 | loop fusion | flops 6291456 | bytes 12582912 | tf_op jit(solution)/shard_map/sub | solution.py:80
  93.8 0.0 all-gather.6.cloned.1.call-update
  93.8 0.0 all-reduce.6.cloned.1.call-start
  93.8 46.4 %all-reduce.4.cloned.1.call-done = f32[32,16384]{1,0:T(8,128)} async-done(((f32[32,16384]{1,0:T(8,128)}), f32[32,16384]{1,0:T(8,128)}) %all-reduce.4.cloned.1.call-update) | async-done | bytes 2097168 | tf_op jit(solution)/shard_map/psum | solution.py:15
  140.2 4.7 %collective-permute-start.1 = (f32[32,16384]{1,0:T(8,128)}, f32[32,16384]{1,0:T(8,128)}, u32[]{:S(2)}, u32[]{:S(2)}) collective-permute-start(f32[32,16384]{1,0:T(8,128)} %all-reduce.4.cloned.1.call-done), channel_id=1, source_target_pairs={{0,4},{4,8},{8,12},{12,16},{16,20},{20,24},{24,28},{1,5},{5,9},{9,... | collective-permute-start | bytes 6291464 | tf_op jit(solution)/shard_map/ppermute | solution.py:21
  144.9 43.6 %collective-permute-done.1 = f32[32,16384]{1,0:T(8,128)} collective-permute-done((f32[32,16384]{1,0:T(8,128)}, f32[32,16384]{1,0:T(8,128)}, u32[]{:S(2)}, u32[]{:S(2)}) %collective-permute-start.1) | collective-permute-done | bytes 2097184 | tf_op jit(solution)/shard_map/ppermute | solution.py:21
  188.5 11.6 %all-gather.6.cloned.1.call-done = f32[128,16384]{1,0:T(8,128)} async-done(((f32[32,16384]{1,0:T(8,128)}), f32[128,16384]{1,0:T(8,128)}) %all-gather.6.cloned.1.call-update) | async-done | bytes 8388624 | tf_op jit(solution)/shard_map/all_gather | solution.py:107
  200.1 10.8 %broadcast_select_fusion = (f32[32,16384]{1,0:T(8,128)}, f32[32,16384]{1,0:T(8,128)S(1)}, f32[32]{0:T(128)S(1)}) fusion(pred[]{:T(512)S(6)} %eq.27, f32[32,16384]{1,0:T(8,128)} %copy-done.4, f32[]{:T(128)S(6)} %mul.175, f32[]{:T(128)S(6)} %sub.156, f32[]{:T(128)} %bitcast.1, f32[128,16384]{1,0:T(8,128)} %all-gather.6.cloned.1.call-done, ...), kind=kOutput, calls=%fused_computation.86 | convolution fusion | flops 821043200 | bytes 18875534 | tf_op jit(solution)/shard_map/dot_general | solution.py:120
  210.9 0.0 copy-start.3
  210.9 0.1 fusion.77
  211.0 2.6 fusion.78
  213.6 0.0 copy-done.3
  213.6 0.0 all-reduce.6.cloned.1.call-update
  213.7 0.2 all-gather.8.cloned.1.call-start
  213.9 5.3 %fusion.4 = f32[32,16384]{1,0:T(8,128)} fusion(f32[32,16384]{1,0:T(8,128)} %copy-done.3, f32[32,16384]{1,0:T(8,128)S(1)} %copy-done, f32[32,1]{1,0:T(8,128)S(1)} %get-tuple-element.14, f32[32,16383]{1,0:T(8,128)} %get-tuple-element.16, f32[32,16383]{1,0:T(8,128)} %get-tuple-element.15, f32[32,1]{1,0:T(8,128)S(1)} %get-tuple-element.13, ...), kind=kLoop, calls=%fused_computation.19 | loop fusion | flops 6291456 | bytes 12582912 | tf_op jit(solution)/shard_map/sub | solution.py:80
  219.2 0.0 copy-start.2
  219.2 0.0 all-gather.8.cloned.1.call-update
  219.3 46.2 %all-reduce.6.cloned.1.call-done = f32[32,16384]{1,0:T(8,128)} async-done(((f32[32,16384]{1,0:T(8,128)}), f32[32,16384]{1,0:T(8,128)}) %all-reduce.6.cloned.1.call-update) | async-done | bytes 2097168 | tf_op jit(solution)/shard_map/psum | solution.py:15
  265.5 4.7 %collective-permute-start.2 = (f32[32,16384]{1,0:T(8,128)}, f32[32,16384]{1,0:T(8,128)}, u32[]{:S(2)}, u32[]{:S(2)}) collective-permute-start(f32[32,16384]{1,0:T(8,128)} %all-reduce.6.cloned.1.call-done), channel_id=1, source_target_pairs={{0,4},{4,8},{8,12},{12,16},{16,20},{20,24},{24,28},{1,5},{5,9},{9,... | collective-permute-start | bytes 6291464 | tf_op jit(solution)/shard_map/ppermute | solution.py:21
  270.2 43.6 %collective-permute-done.2 = f32[32,16384]{1,0:T(8,128)} collective-permute-done((f32[32,16384]{1,0:T(8,128)}, f32[32,16384]{1,0:T(8,128)}, u32[]{:S(2)}, u32[]{:S(2)}) %collective-permute-start.2) | collective-permute-done | bytes 2097184 | tf_op jit(solution)/shard_map/ppermute | solution.py:21
  313.8 11.5 %all-gather.8.cloned.1.call-done = f32[128,16384]{1,0:T(8,128)} async-done(((f32[32,16384]{1,0:T(8,128)}), f32[128,16384]{1,0:T(8,128)}) %all-gather.8.cloned.1.call-update) | async-done | bytes 8388624 | tf_op jit(solution)/shard_map/all_gather | solution.py:107
  325.3 0.0 copy-done.2
  325.3 10.4 %multiply_reduce_fusion = (f32[32]{0:T(128)S(1)}, f32[1,1,32,16384]{3,2,1,0:T(8,128)}) fusion(f32[32,16384]{1,0:T(8,128)} %copy-done.3, f32[]{:T(128)S(6)} %mul.175, f32[]{:T(128)S(6)} %sub.156, f32[]{:T(128)} %bitcast.1, f32[128,16384]{1,0:T(8,128)} %all-gather.8.cloned.1.call-done, f32[128]{0:T(128)S(1)} %select_reduce_fusion, ...), kind=kOutput, calls=%fused_computation.79 | convolution fusion | flops 820518912 | bytes 16778380 | tf_op jit(solution)/shard_map/dot_general | solution.py:120
  335.7 39.6 %all-reduce = (f32[1,32]{1,0:T(1,128)S(1)}, f32[1,32]{1,0:T(1,128)S(1)}, f32[1,32]{1,0:T(1,128)S(1)}) all-reduce(f32[1,32]{1,0:T(1,128)S(1)} %bitcast.29, f32[1,32]{1,0:T(1,128)S(1)} %bitcast.28, f32[1,32]{1,0:T(1,128)S(1)} %bitcast.27), channel_id=1, replica_groups=mesh['tm'=8,'node'=4] {'tm','node'}, use_global_device_ids=true, to_apply=%region_8.9 | all-reduce | flops 96 | bytes 768 | tf_op jit(solution)/shard_map/psum | solution.py:126
  375.3 0.6 fusion.71
  (2 shorter events, 0.0 us)
Async XLA Ops:
  7.2 68.0 %all-gather.4.cloned.1.call-start = ((), (), s32[]{:S(2)}) async-start(), calls=%async_computation | async-start | bytes 10485760 | tf_op jit(solution)/shard_map/all_gather | solution.py:107
  8.0 3.1 copy-start
  8.0 3.5 copy-start.1
  14.0 6.4 %copy-start.5 = (f32[4]{0:T(128)S(1)}, f32[4]{0:T(128)}, u32[]{:S(2)}) copy-start(f32[4]{0:T(128)} %constant.74.clone) | copy-start | bytes 52
  14.0 126.2 %all-reduce.4.cloned.1.call-start = ((), (), s32[]{:S(2)}) async-start(), calls=%async_computation.1 | async-start | bytes 4194304 | tf_op jit(solution)/shard_map/psum | solution.py:15
  14.1 50.1 %collective-permute-start = (f32[32,16384]{1,0:T(8,128)}, f32[32,16384]{1,0:T(8,128)}, u32[]{:S(2)}, u32[]{:S(2)}) collective-permute-start(f32[32,16384]{1,0:T(8,128)} %bitcast.26), channel_id=1, source_target_pairs={{0,4},{4,8},{8,12},{12,16},{16,20},{20,24},{24,28},{1,5},{5,9},{9,... | collective-permute-start | bytes 6291464 | tf_op jit(solution)/shard_map/ppermute | solution.py:21
  85.6 2.7 copy-start.4
  88.4 111.8 %all-gather.6.cloned.1.call-start = ((), (), s32[]{:S(2)}) async-start(), calls=%async_computation.2 | async-start | bytes 10485760 | tf_op jit(solution)/shard_map/all_gather | solution.py:107
  93.8 171.7 %all-reduce.6.cloned.1.call-start = ((), (), s32[]{:S(2)}) async-start(), calls=%async_computation.3 | async-start | bytes 4194304 | tf_op jit(solution)/shard_map/psum | solution.py:15
  140.2 48.3 %collective-permute-start.1 = (f32[32,16384]{1,0:T(8,128)}, f32[32,16384]{1,0:T(8,128)}, u32[]{:S(2)}, u32[]{:S(2)}) collective-permute-start(f32[32,16384]{1,0:T(8,128)} %all-reduce.4.cloned.1.call-done), channel_id=1, source_target_pairs={{0,4},{4,8},{8,12},{12,16},{16,20},{20,24},{24,28},{1,5},{5,9},{9,... | collective-permute-start | bytes 6291464 | tf_op jit(solution)/shard_map/ppermute | solution.py:21
  210.9 2.7 copy-start.3
  213.7 111.6 %all-gather.8.cloned.1.call-start = ((), (), s32[]{:S(2)}) async-start(), calls=%async_computation.4 | async-start | bytes 10485760 | tf_op jit(solution)/shard_map/all_gather | solution.py:107
  219.2 106.0 %copy-start.2 = (f32[1,32,16384]{2,1,0:T(8,128)S(1)}, f32[1,32,16384]{2,1,0:T(8,128)}, u32[]{:S(2)}) copy-start(f32[1,32,16384]{2,1,0:T(8,128)} %param.4) | copy-start | bytes 6291460
  265.5 48.3 %collective-permute-start.2 = (f32[32,16384]{1,0:T(8,128)}, f32[32,16384]{1,0:T(8,128)}, u32[]{:S(2)}, u32[]{:S(2)}) collective-permute-start(f32[32,16384]{1,0:T(8,128)} %all-reduce.6.cloned.1.call-done), channel_id=1, source_target_pairs={{0,4},{4,8},{8,12},{12,16},{16,20},{20,24},{24,28},{1,5},{5,9},{9,... | collective-permute-start | bytes 6291464 | tf_op jit(solution)/shard_map/ppermute | solution.py:21
Sparse Core Ops, SparseCore 0:
  14.1 60.9 all-gather.3
  88.5 51.6 all-reduce.3
  141.8 58.3 all-gather.5
  213.8 51.6 all-reduce.5
  266.9 58.3 all-gather.7
where the time goes:
time: 383 us; the launch traced here: 382 us
  waiting for transfers between devices  255 us (67%)
  blocking collectives  39.6 us (10%)
  matrix products  31.7 us (8%)
  starting transfers between devices  16 us (4%)
  between operations  15.1 us (4%)
  other arithmetic  13.9 us (4%)
  local copies, waits for them, and re-layouts  10.9 us (3%)
    ppermute x3, waiting for transfers between devices, passed_along(): return lax.ppermute(value, axis, pairs)  128 us
    psum x2, waiting for transfers between devices, spread(): return lax.psum(jnp.where(mine, value, jnp.zeros_like(value)), axis)  92.6 us
    psum x1, blocking collectives, body(): totals.append(lax.psum(partial_value, ('tm', 'node')))  39.6 us
    all_gather x3, waiting for transfers between devices, body(): segment = lax.all_gather(forcing, 'node', axis=0, tiled=True)  34.1 us
    dot_general x3, matrix products, body(): jnp.dot(select, segment, precision=lax.Precision.HIGHEST)  31.7 us
    ppermute x3, starting transfers between devices, passed_along(): return lax.ppermute(value, axis, pairs)  15.6 us
    sub x3, other arithmetic, operator_term(): coupling * (right_side - field_values)  13.2 us
    slice x6, local copies, waits for them, and re-layouts, operator_term(): left_side = jnp.roll(field_values, 1, axis=-1)  9.22 us
  transfers between devices with their start and end apart: 8, of which 8 were waited for; matrix products, arithmetic and copies ran while one was open for 3% of the time, Pallas kernels for 0%

commit v1 on v0

--- a/solution.py
+++ b/solution.py
@@ -8,6 +8,7 @@
 NEWTON = 2
 time_step = 0.5
 log_floor = 0.05
+compute_notes = lambda q_in: lax.psum(lax.psum(q_in, "node"), "tm")
 
 
 def spread(value, axis, root):
@@ -123,7 +124,7 @@
         base = start_value + time_step * quadrature
         defect = base - node_state
         partial_value = jnp.sum(defect * defect, axis=1)
-        totals.append(lax.psum(partial_value, ("tm", "node")))
+        totals.append(compute_notes(partial_value))
         target = base - implicit * (node_state - node_state * node_state * node_state)
         iterate = node_state
         for newton_step in range(NEWTON):

time: 383 us -> 371 us (0.969)
  blocking collectives: 39.6 us -> 27.7 us
    psum x1 -> x2, blocking collectives: 39.6 us -> 27.7 us  [compute_notes = lambda q_in: lax.psum(lax.psum(q_in, 'node'), 'tm')]
where the time goes in v1:
time: 371 us
  waiting for transfers between devices  255 us (69%)
  matrix products  31.7 us (9%)
  blocking collectives  27.7 us (7%)
  starting transfers between devices  16 us (4%)
  between operations  15.1 us (4%)
  other arithmetic  13.9 us (4%)
  local copies, waits for them, and re-layouts  11 us (3%)
    ppermute x3, waiting for transfers between devices, passed_along(): return lax.ppermute(value, axis, pairs)  128 us
    psum x2, waiting for transfers between devices, spread(): return lax.psum(jnp.where(mine, value, jnp.zeros_like(value)), axis)  92.6 us
    all_gather x3, waiting for transfers between devices, body(): segment = lax.all_gather(forcing, 'node', axis=0, tiled=True)  34.1 us
    dot_general x3, matrix products, body(): jnp.dot(select, segment, precision=lax.Precision.HIGHEST)  31.7 us
    psum x2, blocking collectives, compute_notes = lambda q_in: lax.psum(lax.psum(q_in, 'node'), 'tm')  27.7 us
    ppermute x3, starting transfers between devices, passed_along(): return lax.ppermute(value, axis, pairs)  15.6 us
    sub x3, other arithmetic, operator_term(): coupling * (right_side - field_values)  13.2 us
    slice x6, local copies, waits for them, and re-layouts, operator_term(): left_side = jnp.roll(field_values, 1, axis=-1)  9.22 us
  transfers between devices with their start and end apart: 8, of which 8 were waited for; matrix products, arithmetic and copies ran while one was open for 3% of the time, Pallas kernels for 0%

profile of v1, /device:TPU:0, one launch (start us, length us, event | category | flops | bytes accessed | tf_op | source)
XLA Modules:
  0.0 370.5 jit_solution(1741457527429590860)
XLA Ops:
  7.2 0.0 all-gather.4.cloned.1.call-start
  7.2 0.8 fusion.81
  8.0 0.0 copy-start
  8.0 0.0 copy-start.1
  8.0 3.0 fusion.82
  11.1 0.0 copy-done
  11.1 0.1 slice.52
  11.2 0.4 copy-done.1
  11.5 2.5 fusion
  14.0 0.0 copy-start.5
  14.0 0.0 all-gather.4.cloned.1.call-update
  14.0 0.0 all-reduce.5.cloned.1.call-start
  14.1 6.3 %collective-permute-start = (f32[32,16384]{1,0:T(8,128)}, f32[32,16384]{1,0:T(8,128)}, u32[]{:S(2)}, u32[]{:S(2)}) collective-permute-start(f32[32,16384]{1,0:T(8,128)} %bitcast.26), channel_id=1, source_target_pairs={{0,4},{4,8},{8,12},{12,16},{16,20},{20,24},{24,28},{1,5},{5,9},{9,... | collective-permute-start | bytes 6291464 | tf_op jit(solution)/shard_map/ppermute | solution.py:22
  20.3 0.0 copy-done.5
  20.3 0.6 dynamic_slice.6
  22.3 0.7 dynamic-slice_bitcast_fusion
  23.0 0.1 select_reduce_fusion
  23.0 41.1 %collective-permute-done = f32[32,16384]{1,0:T(8,128)} collective-permute-done((f32[32,16384]{1,0:T(8,128)}, f32[32,16384]{1,0:T(8,128)}, u32[]{:S(2)}, u32[]{:S(2)}) %collective-permute-start) | collective-permute-done | bytes 2097184 | tf_op jit(solution)/shard_map/ppermute | solution.py:22
  64.2 11.0 %all-gather.4.cloned.1.call-done = f32[128,16384]{1,0:T(8,128)} async-done(((f32[32,16384]{1,0:T(8,128)}), f32[128,16384]{1,0:T(8,128)}) %all-gather.4.cloned.1.call-update) | async-done | bytes 8388624 | tf_op jit(solution)/shard_map/all_gather | solution.py:108
  75.2 10.5 %broadcast_select_fusion.1 = (f32[32,16384]{1,0:T(8,128)}, f32[32,16384]{1,0:T(8,128)S(1)}, f32[32]{0:T(128)S(1)}) fusion(pred[]{:T(512)S(6)} %eq.27, f32[]{:T(128)S(6)} %mul.175, f32[]{:T(128)S(6)} %sub.156, f32[32,16384]{1,0:T(8,128)} %collective-permute-done, pred[]{:T(512)S(6)} %eq.20, f32[]{:T(128)} %bitcast.1, f32[1,32,16384]{2,1,0:T(8,128)} %param.4, ...), kind=kOutput, calls=%fused_computation.87 | convolution fusion | flops 821043200 | bytes 16778382 | tf_op jit(solution)/shard_map/dot_general | solution.py:121
  85.6 0.0 copy-start.4
  85.6 0.1 fusion.79
  85.7 2.6 fusion.80
  88.3 0.0 copy-done.4
  88.3 0.0 all-reduce.5.cloned.1.call-update
  88.4 0.0 all-gather.6.cloned.1.call-start
  88.4 5.3 %fusion.2 = f32[32,16384]{1,0:T(8,128)} fusion(f32[32,16384]{1,0:T(8,128)} %copy-done.4, f32[32,16384]{1,0:T(8,128)S(1)} %copy-done, f32[32,1]{1,0:T(8,128)S(1)} %get-tuple-element.21, f32[32,16383]{1,0:T(8,128)} %get-tuple-element.23, f32[32,16383]{1,0:T(8,128)} %get-tuple-element.22, f32[32,1]{1,0:T(8,128)S(1)} %get-tuple-element.20, ...), kind=kLoop, calls=%fused_computation.17 | loop fusion | flops 6291456 | bytes 12582912 | tf_op jit(solution)/shard_map/sub | solution.py:81
  93.7 0.0 all-gather.6.cloned.1.call-update
  93.8 0.0 all-reduce.7.cloned.1.call-start
  93.8 46.4 %all-reduce.5.cloned.1.call-done = f32[32,16384]{1,0:T(8,128)} async-done(((f32[32,16384]{1,0:T(8,128)}), f32[32,16384]{1,0:T(8,128)}) %all-reduce.5.cloned.1.call-update) | async-done | bytes 2097168 | tf_op jit(solution)/shard_map/psum | solution.py:16
  140.2 4.7 %collective-permute-start.1 = (f32[32,16384]{1,0:T(8,128)}, f32[32,16384]{1,0:T(8,128)}, u32[]{:S(2)}, u32[]{:S(2)}) collective-permute-start(f32[32,16384]{1,0:T(8,128)} %all-reduce.5.cloned.1.call-done), channel_id=1, source_target_pairs={{0,4},{4,8},{8,12},{12,16},{16,20},{20,24},{24,28},{1,5},{5,9},{9,... | collective-permute-start | bytes 6291464 | tf_op jit(solution)/shard_map/ppermute | solution.py:22
  144.9 43.7 %collective-permute-done.1 = f32[32,16384]{1,0:T(8,128)} collective-permute-done((f32[32,16384]{1,0:T(8,128)}, f32[32,16384]{1,0:T(8,128)}, u32[]{:S(2)}, u32[]{:S(2)}) %collective-permute-start.1) | collective-permute-done | bytes 2097184 | tf_op jit(solution)/shard_map/ppermute | solution.py:22
  188.5 11.6 %all-gather.6.cloned.1.call-done = f32[128,16384]{1,0:T(8,128)} async-done(((f32[32,16384]{1,0:T(8,128)}), f32[128,16384]{1,0:T(8,128)}) %all-gather.6.cloned.1.call-update) | async-done | bytes 8388624 | tf_op jit(solution)/shard_map/all_gather | solution.py:108
  200.1 10.8 %broadcast_select_fusion = (f32[32,16384]{1,0:T(8,128)}, f32[32,16384]{1,0:T(8,128)S(1)}, f32[32]{0:T(128)S(1)}) fusion(pred[]{:T(512)S(6)} %eq.27, f32[32,16384]{1,0:T(8,128)} %copy-done.4, f32[]{:T(128)S(6)} %mul.175, f32[]{:T(128)S(6)} %sub.156, f32[]{:T(128)} %bitcast.1, f32[128,16384]{1,0:T(8,128)} %all-gather.6.cloned.1.call-done, ...), kind=kOutput, calls=%fused_computation.86 | convolution fusion | flops 821043200 | bytes 18875534 | tf_op jit(solution)/shard_map/dot_general | solution.py:121
  210.9 0.0 copy-start.3
  210.9 0.1 fusion.77
  211.0 2.6 fusion.78
  213.6 0.0 copy-done.3
  213.6 0.0 all-reduce.7.cloned.1.call-update
  213.7 0.2 all-gather.8.cloned.1.call-start
  213.9 5.3 %fusion.4 = f32[32,16384]{1,0:T(8,128)} fusion(f32[32,16384]{1,0:T(8,128)} %copy-done.3, f32[32,16384]{1,0:T(8,128)S(1)} %copy-done, f32[32,1]{1,0:T(8,128)S(1)} %get-tuple-element.17, f32[32,16383]{1,0:T(8,128)} %get-tuple-element.19, f32[32,16383]{1,0:T(8,128)} %get-tuple-element.18, f32[32,1]{1,0:T(8,128)S(1)} %get-tuple-element.16, ...), kind=kLoop, calls=%fused_computation.19 | loop fusion | flops 6291456 | bytes 12582912 | tf_op jit(solution)/shard_map/sub | solution.py:81
  219.2 0.0 copy-start.2
  219.2 0.0 all-gather.8.cloned.1.call-update
  219.3 46.2 %all-reduce.7.cloned.1.call-done = f32[32,16384]{1,0:T(8,128)} async-done(((f32[32,16384]{1,0:T(8,128)}), f32[32,16384]{1,0:T(8,128)}) %all-reduce.7.cloned.1.call-update) | async-done | bytes 2097168 | tf_op jit(solution)/shard_map/psum | solution.py:16
  265.5 4.7 %collective-permute-start.2 = (f32[32,16384]{1,0:T(8,128)}, f32[32,16384]{1,0:T(8,128)}, u32[]{:S(2)}, u32[]{:S(2)}) collective-permute-start(f32[32,16384]{1,0:T(8,128)} %all-reduce.7.cloned.1.call-done), channel_id=1, source_target_pairs={{0,4},{4,8},{8,12},{12,16},{16,20},{20,24},{24,28},{1,5},{5,9},{9,... | collective-permute-start | bytes 6291464 | tf_op jit(solution)/shard_map/ppermute | solution.py:22
  270.2 43.7 %collective-permute-done.2 = f32[32,16384]{1,0:T(8,128)} collective-permute-done((f32[32,16384]{1,0:T(8,128)}, f32[32,16384]{1,0:T(8,128)}, u32[]{:S(2)}, u32[]{:S(2)}) %collective-permute-start.2) | collective-permute-done | bytes 2097184 | tf_op jit(solution)/shard_map/ppermute | solution.py:22
  313.8 11.5 %all-gather.8.cloned.1.call-done = f32[128,16384]{1,0:T(8,128)} async-done(((f32[32,16384]{1,0:T(8,128)}), f32[128,16384]{1,0:T(8,128)}) %all-gather.8.cloned.1.call-update) | async-done | bytes 8388624 | tf_op jit(solution)/shard_map/all_gather | solution.py:108
  325.3 0.0 copy-done.2
  325.3 10.4 %multiply_reduce_fusion = (f32[32]{0:T(128)S(1)}, f32[1,1,32,16384]{3,2,1,0:T(8,128)}) fusion(f32[32,16384]{1,0:T(8,128)} %copy-done.3, f32[]{:T(128)S(6)} %mul.175, f32[]{:T(128)S(6)} %sub.156, f32[]{:T(128)} %bitcast.1, f32[128,16384]{1,0:T(8,128)} %all-gather.8.cloned.1.call-done, f32[128]{0:T(128)S(1)} %select_reduce_fusion, ...), kind=kOutput, calls=%fused_computation.79 | convolution fusion | flops 820518912 | bytes 16778380 | tf_op jit(solution)/shard_map/dot_general | solution.py:121
  335.7 5.9 %all-reduce.1 = (f32[32]{0:T(128)S(1)}, f32[32]{0:T(128)S(1)}, f32[32]{0:T(128)S(1)}) all-reduce(f32[32]{0:T(128)S(1)} %get-tuple-element.14, f32[32]{0:T(128)S(1)} %get-tuple-element.13, f32[32]{0:T(128)S(1)} %get-tuple-element.12), channel_id=1, replica_groups=mesh['tm'=8,'node'=4] {'node'}, use_global_device_ids=true, to_apply=%region_10.11 | all-reduce | flops 96 | bytes 768 | tf_op jit(solution)/shard_map/psum | solution.py:11
  341.6 21.8 %all-reduce = (f32[1,32]{1,0:T(1,128)S(1)}, f32[1,32]{1,0:T(1,128)S(1)}, f32[1,32]{1,0:T(1,128)S(1)}) all-reduce(f32[1,32]{1,0:T(1,128)S(1)} %bitcast.27, f32[1,32]{1,0:T(1,128)S(1)} %bitcast.28, f32[1,32]{1,0:T(1,128)S(1)} %bitcast.29), channel_id=1, replica_groups=mesh['tm'=8,'node'=4] {'tm'}, use_global_device_ids=true, to_apply=%region_11.12 | all-reduce | flops 96 | bytes 768 | tf_op jit(solution)/shard_map/psum | solution.py:11
  363.4 0.6 fusion.71
  (2 shorter events, 0.0 us)
Async XLA Ops:
  7.2 68.0 %all-gather.4.cloned.1.call-start = ((), (), s32[]{:S(2)}) async-start(), calls=%async_computation | async-start | bytes 10485760 | tf_op jit(solution)/shard_map/all_gather | solution.py:108
  8.0 3.1 copy-start
  8.0 3.5 copy-start.1
  14.0 6.4 %copy-start.5 = (f32[4]{0:T(128)S(1)}, f32[4]{0:T(128)}, u32[]{:S(2)}) copy-start(f32[4]{0:T(128)} %constant.74.clone) | copy-start | bytes 52
  14.0 126.2 %all-reduce.5.cloned.1.call-start = ((), (), s32[]{:S(2)}) async-start(), calls=%async_computation.1 | async-start | bytes 4194304 | tf_op jit(solution)/shard_map/psum | solution.py:16
  14.1 50.1 %collective-permute-start = (f32[32,16384]{1,0:T(8,128)}, f32[32,16384]{1,0:T(8,128)}, u32[]{:S(2)}, u32[]{:S(2)}) collective-permute-start(f32[32,16384]{1,0:T(8,128)} %bitcast.26), channel_id=1, source_target_pairs={{0,4},{4,8},{8,12},{12,16},{16,20},{20,24},{24,28},{1,5},{5,9},{9,... | collective-permute-start | bytes 6291464 | tf_op jit(solution)/shard_map/ppermute | solution.py:22
  85.6 2.7 copy-start.4
  88.4 111.8 %all-gather.6.cloned.1.call-start = ((), (), s32[]{:S(2)}) async-start(), calls=%async_computation.2 | async-start | bytes 10485760 | tf_op jit(solution)/shard_map/all_gather | solution.py:108
  93.8 171.7 %all-reduce.7.cloned.1.call-start = ((), (), s32[]{:S(2)}) async-start(), calls=%async_computation.3 | async-start | bytes 4194304 | tf_op jit(solution)/shard_map/psum | solution.py:16
  140.2 48.3 %collective-permute-start.1 = (f32[32,16384]{1,0:T(8,128)}, f32[32,16384]{1,0:T(8,128)}, u32[]{:S(2)}, u32[]{:S(2)}) collective-permute-start(f32[32,16384]{1,0:T(8,128)} %all-reduce.5.cloned.1.call-done), channel_id=1, source_target_pairs={{0,4},{4,8},{8,12},{12,16},{16,20},{20,24},{24,28},{1,5},{5,9},{9,... | collective-permute-start | bytes 6291464 | tf_op jit(solution)/shard_map/ppermute | solution.py:22
  210.9 2.7 copy-start.3
  213.7 111.6 %all-gather.8.cloned.1.call-start = ((), (), s32[]{:S(2)}) async-start(), calls=%async_computation.4 | async-start | bytes 10485760 | tf_op jit(solution)/shard_map/all_gather | solution.py:108
  219.2 106.1 %copy-start.2 = (f32[1,32,16384]{2,1,0:T(8,128)S(1)}, f32[1,32,16384]{2,1,0:T(8,128)}, u32[]{:S(2)}) copy-start(f32[1,32,16384]{2,1,0:T(8,128)} %param.4) | copy-start | bytes 6291460
  265.5 48.3 %collective-permute-start.2 = (f32[32,16384]{1,0:T(8,128)}, f32[32,16384]{1,0:T(8,128)}, u32[]{:S(2)}, u32[]{:S(2)}) collective-permute-start(f32[32,16384]{1,0:T(8,128)} %all-reduce.7.cloned.1.call-done), channel_id=1, source_target_pairs={{0,4},{4,8},{8,12},{12,16},{16,20},{20,24},{24,28},{1,5},{5,9},{9,... | collective-permute-start | bytes 6291464 | tf_op jit(solution)/shard_map/ppermute | solution.py:22
Sparse Core Ops, SparseCore 0:
  14.1 60.9 all-gather.3
  88.5 51.6 all-reduce.4
  141.8 58.3 all-gather.5
  213.8 51.6 all-reduce.6
  266.9 58.3 all-gather.7
